TPU v7x, 32 devices: a whole 2x2x4 slice. The times are simulated.
32 devices in a mesh: vocab: 8 (over z, x), tok: 4 (over y, core).
Axes of the slice: x: 2, y: 2, z: 4, core: 2. Of those that a mesh axis runs over, the one named last changes fastest.
Arguments:
- hidden: bfloat16 [768, 7168], P('tok', 'vocab'), may hold values from -21 to 21
- head_weight: bfloat16 [7168, 8192], P('tok', 'vocab'), may hold values from -0.12695312 to 0.12695312
- targets: int32 [768], P('tok'), may hold values from 0 to 6143
- vocab_mask: int32 [8192], P('vocab'), may hold values from 0 to 1, as said below
- token_grad: float32 [768], P('tok'), may hold values from 16 to 160
Outputs:
- hidden_grad: bfloat16 [768, 7168], P('tok', 'vocab')
- token_loss: float32 [768], P('tok')
Inputs may be any that keep to these rules, and one draw needn't show every extreme that they name: vocab_mask is 1 on the columns below some cut and 0 from it on, with between 1 and 2048 zeros.
All inputs are finite; a program needn't handle non-finite values.
Results may differ from a plain program's by a relative error of at most 0.0051.
Values may be sent and summed in bfloat16 or wider, within the bound.
A program may use at most 64 MiB of HBM per device.

v0:
```python
import jax
import jax.numpy as jnp
from jax import lax
from jax.sharding import PartitionSpec as P


def combined_all(value, axis, join):
    pieces = jax.tree.map(lambda part: lax.all_gather(part, axis), value)
    head = jax.tree.map(lambda part: part[0], pieces)
    tail = jax.tree.map(lambda part: part[1:], pieces)
    running, _ = lax.scan(lambda running, share: (join(running, share), None), head, tail)
    return running


def combine_pairs(left_part, right_part):
    larger = jnp.maximum(left_part[0], right_part[0])
    summed = left_part[1] * jnp.exp(left_part[0] - larger) + right_part[1] * jnp.exp(
        right_part[0] - larger
    )
    return (larger, summed, left_part[2] + right_part[2])


def on_device(hidden, head_weight, targets, vocab_mask, token_grad):
    gathered = lax.all_gather(hidden, "vocab", axis=1, tiled=True)
    block_width = head_weight.shape[1]
    first_column = lax.axis_index("vocab") * block_width
    logits = jnp.dot(
        gathered,
        lax.all_gather(head_weight, "tok", axis=0, tiled=True),
        preferred_element_type=jnp.float32,
    )
    live_mask = vocab_mask[None, :] == 1
    masked = jnp.where(live_mask, logits, jnp.float32(-1e30))
    local_max = jnp.max(masked, axis=1)
    columns = first_column + jnp.arange(block_width, dtype=jnp.int32)
    onehot = columns[None, :] == targets[:, None]
    local_target = jnp.sum(jnp.where(onehot, logits, jnp.float32(0.0)), axis=1)
    local_sum = jnp.sum(jnp.exp(masked - local_max[:, None]), axis=1)
    row_max, denominator, target_logit = combined_all(
        (local_max, local_sum, local_target), "vocab", combine_pairs
    )
    log_norm = row_max + jnp.log(denominator)
    token_loss = log_norm - target_logit
    probabilities = jnp.exp(masked - log_norm[:, None])
    logit_grad = (token_grad[:, None] * (probabilities - onehot.astype(jnp.float32))).astype(
        jnp.bfloat16
    )
    partial_value = lax.dot_general(
        logit_grad,
        lax.all_gather(head_weight, "tok", axis=0, tiled=True),
        (((1,), (1,)), ((), ())),
        preferred_element_type=jnp.float32,
    )
    hidden_grad = lax.psum_scatter(partial_value, "vocab", scatter_dimension=1, tiled=True).astype(
        jnp.bfloat16
    )
    return (hidden_grad, token_loss)


def solution(mesh):
    placed = (P("tok", "vocab"), P("tok", "vocab"), P("tok"), P("vocab"), P("tok"))
    return jax.shard_map(
        on_device,
        mesh=mesh,
        in_specs=placed,
        out_specs=(P("tok", "vocab"), P("tok")),
        check_vma=False,
    )
```

profile of v0, /device:TPU:0, one launch (start us, length us, event | category | flops | bytes accessed | tf_op | source)
XLA Modules:
  0.0 334.8 jit_solution(9599591068299161233)
XLA Ops:
  7.2 0.0 all-gather.6.cloned.1.call-start
  7.2 0.7 all-gather.6.cloned.1.call-update
  7.9 0.0 all-gather.8.cloned.1.call-start
  7.9 0.7 all-gather.8.cloned.1.call-update
  8.6 0.0 copy-start
  8.7 0.0 reduce-scatter.2.cloned.1.call-start
  8.7 1.2 dynamic-slice
  10.6 0.7 broadcast_compare_fusion
  11.3 0.0 copy-start.1
  11.3 57.9 %all-gather.6.cloned.1.call-done = bf16[192,7168]{1,0:T(8,128)(2,1)} async-done(((bf16[192,896]{1,0:T(8,128)(2,1)}), bf16[192,7168]{1,0:T(8,128)(2,1)}) %all-gather.6.cloned.1.call-update) | async-done | bytes 2752528 | tf_op jit(solution)/shard_map/all_gather | solution.py:24
  69.2 93.7 %all-gather.8.cloned.1.call-done = bf16[7168,1024]{1,0:T(8,128)(2,1)} async-done(((bf16[1792,1024]{1,0:T(8,128)(2,1)}), bf16[7168,1024]{1,0:T(8,128)(2,1)}) %all-gather.8.cloned.1.call-update) | async-done | bytes 14680080 | tf_op jit(solution)/shard_map/all_gather | solution.py:29
  162.9 7.7 %select_reduce_fusion = (f32[192]{0:T(256)S(1)}, f32[192,1024]{1,0:T(8,128)S(1)}) fusion(pred[1024]{0:T(1024)(128)(4,1)S(1)} %broadcast_compare_fusion, bf16[192,7168]{1,0:T(8,128)(2,1)} %all-gather.6.cloned.1.call-done, bf16[7168,1024]{1,0:T(8,128)(2,1)} %all-gather.8.cloned.1.call-done), kind=kOutput, calls=%fused_computation.11 | convolution fusion | flops 2818965248 | bytes 18220800 | tf_op jit(solution)/shard_map/dot_general | solution.py:27
  170.6 0.3 dynamic-update-slice
  170.9 0.0 copy-done
  170.9 0.4 fusion
  171.3 0.3 dynamic-update-slice.1
  171.6 0.3 dynamic-update-slice.2
  171.8 37.0 %all-reduce.3 = (f32[1536]{0:T(1024)S(1)}, f32[1536]{0:T(1024)S(1)}, f32[1536]{0:T(1024)S(1)}) all-reduce(f32[1536]{0:T(1024)S(1)} %dynamic-update-slice, f32[1536]{0:T(1024)S(1)} %dynamic-update-slice.1, f32[1536]{0:T(1024)S(1)} %dynamic-update-slice.2), channel_id=2, replica_groups=mesh['vocab'=8,'tok'=4] {'vocab'}, use_global_device_ids=true, to_apply=%add | all-reduce | flops 4608 | bytes 36864
  208.8 0.1 slice.33
  208.9 0.1 slice.34
  209.0 0.1 slice.35
  209.0 0.1 reshape.23
  209.1 0.1 reshape.24
  209.2 0.1 reshape.25
  209.3 0.6 while.14
  209.8 0.6 fusion.13
  210.4 0.0 copy-done.1
  210.4 12.6 %fusion.4 = f32[192,7168]{1,0:T(8,128)} fusion(bf16[7168,1024]{1,0:T(8,128)(2,1)} %all-gather.8.cloned.1.call-done, f32[192,1024]{1,0:T(8,128)S(1)} %get-tuple-element.70, f32[192]{0:T(256)S(1)} %get-tuple-element.66, s32[1024]{0:T(1024)S(1)} %iota_add_fusion, f32[192]{0:T(256)S(1)} %copy-done.1, s32[192]{0:T(256)S(1)} %copy-done, ...), kind=kOutput, calls=%fused_computation.12 | convolution fusion | flops 2819948544 | bytes 20978944 | tf_op jit(solution)/shard_map/dot_general | solution.py:48
  223.0 0.0 reduce-scatter.2.cloned.1.call-update
  223.0 103.4 %reduce-scatter.2.cloned.1.call-done = f32[192,896]{1,0:T(8,128)} async-done(((f32[192,7168]{1,0:T(8,128)}), f32[192,896]{1,0:T(8,128)}) %reduce-scatter.2.cloned.1.call-update) | async-done | bytes 688144 | tf_op jit(solution)/shard_map/reduce_scatter | solution.py:54
  326.4 1.9 convert_element_type.11
  (35 shorter events, 0.4 us)
Async XLA Ops:
  7.2 62.1 %all-gather.6.cloned.1.call-start = ((), (), s32[]{:S(2)}) async-start(), calls=%async_computation.1 | async-start | bytes 3096576 | tf_op jit(solution)/shard_map/all_gather | solution.py:24
  7.9 155.1 %all-gather.8.cloned.1.call-start = ((), (), s32[]{:S(2)}) async-start(), calls=%async_computation.2 | async-start | bytes 18350080 | tf_op jit(solution)/shard_map/all_gather | solution.py:29
  8.6 162.3 %copy-start = (s32[192]{0:T(256)S(1)}, s32[192]{0:T(256)}, u32[]{:S(2)}) copy-start(s32[192]{0:T(256)} %param.9) | copy-start | bytes 2308
  8.7 317.8 %reduce-scatter.2.cloned.1.call-start = ((), (), s32[]{:S(2)}) async-start(), calls=%async_computation.3 | async-start | bytes 6193152 | tf_op jit(solution)/shard_map/reduce_scatter | solution.py:54
  11.3 199.1 %copy-start.1 = (f32[192]{0:T(256)S(1)}, f32[192]{0:T(256)}, u32[]{:S(2)}) copy-start(f32[192]{0:T(256)} %param.11) | copy-start | bytes 2308
Sparse Core Ops, SparseCore 0:
  10.1 59.0 all-gather.5
  70.8 92.1 all-gather.7
  223.1 103.2 reduce-scatter.1
where the time goes:
time: 335 us
  waiting for transfers between devices  256 us (76%)
  blocking collectives  37 us (11%)
  matrix products  20.3 us (6%)
  between operations  14.5 us (4%)
  other arithmetic  3.74 us (1%)
    reduce_scatter x1, waiting for transfers between devices, on_device(): lax.psum_scatter(partial_value, 'vocab', scatter_dimension=1, tiled=True)  103 us
    all_gather x1, waiting for transfers between devices, on_device(): lax.all_gather(head_weight, 'tok', axis=0, tiled=True)  93.7 us
    all_gather x1, waiting for transfers between devices, on_device(): gathered = lax.all_gather(hidden, 'vocab', axis=1, tiled=True)  57.9 us
    unnamed x1, blocking collectives  37 us
    dot_general x1, matrix products, on_device(): lax.dot_general(logit_grad, lax.all_gather(head_weight, 'tok', axis=0, ti...  12.6 us
    dot_general x1, matrix products, on_device(): jnp.dot(gathered, lax.all_gather(head_weight, 'tok', axis=0, tiled=True),...  7.66 us
  transfers between devices with their start and end apart: 3, of which 3 were waited for; matrix products, arithmetic and copies ran while one was open for 1% of the time, Pallas kernels for 0%

commit v1 on v0

--- a/solution.py
+++ b/solution.py
@@ -21,7 +21,14 @@
 
 
 def on_device(hidden, head_weight, targets, vocab_mask, token_grad):
-    gathered = lax.all_gather(hidden, "vocab", axis=1, tiled=True)
+    ring = [hidden]
+    for hop in range(7):
+        ring.append(lax.ppermute(ring[-1], "vocab", [(dev, (dev + 1) % 8) for dev in range(8)]))
+    gathered = jnp.roll(
+        jnp.concatenate(ring[::-1], axis=1),
+        (lax.axis_index("vocab") + 1) * ring[0].shape[1],
+        axis=1,
+    )
     block_width = head_weight.shape[1]
     first_column = lax.axis_index("vocab") * block_width
     logits = jnp.dot(

time: 335 us -> 279 us (0.83)
  waiting for transfers between devices: 256 us -> 184 us
  local copies, waits for them, and re-layouts: 2.65 us -> 15.2 us
    all_gather x1, waiting for transfers between devices: 93.7 us -> 8.11 us  [on_device(): lax.all_gather(head_weight, 'tok', axis=0, tiled=True)]
    ppermute x0 -> x7, waiting for transfers between devices: none -> 72 us  [on_device(): lax.ppermute(ring[-1], 'vocab', [(dev, (dev + 1) % 8) for dev in range(8)])]
    all_gather x1 -> x0, waiting for transfers between devices: 57.9 us -> none  [on_device(): gathered = lax.all_gather(hidden, 'vocab', axis=1, tiled=True)]
    unnamed x11 -> x28, local copies, waits for them, and re-layouts: 2.07 us -> 13.8 us
  transfers between devices with their start and end apart: 3 -> 9, of which waited for: 3 -> 9; matrix products, arithmetic and copies ran while one was open for 1% -> 5% of each run, Pallas kernels for 0% -> 0%
where the time goes in v1:
time: 279 us
  waiting for transfers between devices  184 us (66%)
  blocking collectives  37 us (13%)
  matrix products  20.3 us (7%)
  local copies, waits for them, and re-layouts  15.2 us (5%)
  between operations  14.8 us (5%)
  other arithmetic  3.73 us (1%)
  starting transfers between devices  3.11 us (1%)
    reduce_scatter x1, waiting for transfers between devices, on_device(): lax.psum_scatter(partial_value, 'vocab', scatter_dimension=1, tiled=True)  103 us
    ppermute x7, waiting for transfers between devices, on_device(): lax.ppermute(ring[-1], 'vocab', [(dev, (dev + 1) % 8) for dev in range(8)])  72 us
    unnamed x1, blocking collectives  37 us
    unnamed x28, local copies, waits for them, and re-layouts  13.8 us
    dot_general x1, matrix products, on_device(): lax.dot_general(logit_grad, lax.all_gather(head_weight, 'tok', axis=0, ti...  12.6 us
    all_gather x1, waiting for transfers between devices, on_device(): lax.all_gather(head_weight, 'tok', axis=0, tiled=True)  8.11 us
    dot_general x1, matrix products, on_device(): jnp.dot(gathered, lax.all_gather(head_weight, 'tok', axis=0, tiled=True),...  7.72 us
  transfers between devices with their start and end apart: 9, of which 9 were waited for; matrix products, arithmetic and copies ran while one was open for 5% of the time, Pallas kernels for 0%

profile of v1, /device:TPU:0, one launch (start us, length us, event | category | flops | bytes accessed | tf_op | source)
XLA Modules:
  0.0 278.5 jit_solution(2367670656066571214)
XLA Ops:
  8.0 3.0 %collective-permute-start = (bf16[192,896]{1,0:T(8,128)(2,1)}, bf16[192,896]{1,0:T(8,128)(2,1)S(1)}, u32[]{:S(2)}, u32[]{:S(2)}) collective-permute-start(bf16[192,896]{1,0:T(8,128)(2,1)} %param.7), channel_id=1, source_target_pairs={{0,4},{4,8},{8,12},{12,16},{16,20},{20,24},{24,28},{28,0},{1,5},{5... | collective-permute-start | bytes 1032200 | tf_op jit(solution)/shard_map/ppermute | solution.py:26
  11.0 11.3 %collective-permute-done = bf16[192,896]{1,0:T(8,128)(2,1)S(1)} collective-permute-done((bf16[192,896]{1,0:T(8,128)(2,1)}, bf16[192,896]{1,0:T(8,128)(2,1)S(1)}, u32[]{:S(2)}, u32[]{:S(2)}) %collective-permute-start) | collective-permute-done | bytes 344096 | tf_op jit(solution)/shard_map/ppermute | solution.py:26
  22.3 11.9 %collective-permute-done.1 = bf16[192,896]{1,0:T(8,128)(2,1)S(1)} collective-permute-done((bf16[192,896]{1,0:T(8,128)(2,1)S(1)}, bf16[192,896]{1,0:T(8,128)(2,1)S(1)}, u32[]{:S(2)}, u32[]{:S(2)}) %collective-permute-start.1) | collective-permute-done | bytes 344096 | tf_op jit(solution)/shard_map/ppermute | solution.py:26
  34.2 11.1 %collective-permute-done.2 = bf16[192,896]{1,0:T(8,128)(2,1)S(1)} collective-permute-done((bf16[192,896]{1,0:T(8,128)(2,1)S(1)}, bf16[192,896]{1,0:T(8,128)(2,1)S(1)}, u32[]{:S(2)}, u32[]{:S(2)}) %collective-permute-start.2) | collective-permute-done | bytes 344096 | tf_op jit(solution)/shard_map/ppermute | solution.py:26
  45.3 10.2 %collective-permute-done.3 = bf16[192,896]{1,0:T(8,128)(2,1)S(1)} collective-permute-done((bf16[192,896]{1,0:T(8,128)(2,1)S(1)}, bf16[192,896]{1,0:T(8,128)(2,1)S(1)}, u32[]{:S(2)}, u32[]{:S(2)}) %collective-permute-start.3) | collective-permute-done | bytes 344096 | tf_op jit(solution)/shard_map/ppermute | solution.py:26
  55.5 9.9 %collective-permute-done.4 = bf16[192,896]{1,0:T(8,128)(2,1)S(1)} collective-permute-done((bf16[192,896]{1,0:T(8,128)(2,1)S(1)}, bf16[192,896]{1,0:T(8,128)(2,1)S(1)}, u32[]{:S(2)}, u32[]{:S(2)}) %collective-permute-start.4) | collective-permute-done | bytes 344096 | tf_op jit(solution)/shard_map/ppermute | solution.py:26
  65.4 10.3 %collective-permute-done.5 = bf16[192,896]{1,0:T(8,128)(2,1)S(1)} collective-permute-done((bf16[192,896]{1,0:T(8,128)(2,1)S(1)}, bf16[192,896]{1,0:T(8,128)(2,1)S(1)}, u32[]{:S(2)}, u32[]{:S(2)}) %collective-permute-start.5) | collective-permute-done | bytes 344096 | tf_op jit(solution)/shard_map/ppermute | solution.py:26
  75.7 1.2 dynamic-slice
  77.6 0.7 broadcast_compare_fusion
  78.3 7.3 %collective-permute-done.6 = bf16[192,896]{1,0:T(8,128)(2,1)S(1)} collective-permute-done((bf16[192,896]{1,0:T(8,128)(2,1)S(1)}, bf16[192,896]{1,0:T(8,128)(2,1)S(1)}, u32[]{:S(2)}, u32[]{:S(2)}) %collective-permute-start.6) | collective-permute-done | bytes 344096 | tf_op jit(solution)/shard_map/ppermute | solution.py:26
  85.6 0.8 constant_dynamic-update-slice_fusion.15
  86.4 0.8 constant_dynamic-update-slice_fusion.14
  87.2 0.8 constant_dynamic-update-slice_fusion.13
  88.0 0.8 constant_dynamic-update-slice_fusion.12
  88.8 0.8 constant_dynamic-update-slice_fusion.11
  89.6 0.8 constant_dynamic-update-slice_fusion.10
  90.4 0.8 constant_dynamic-update-slice_fusion.9
  91.1 0.8 constant_dynamic-update-slice_fusion.8
  91.9 0.8 constant_dynamic-update-slice_fusion.7
  92.7 0.8 constant_dynamic-update-slice_fusion.6
  93.5 0.8 constant_dynamic-update-slice_fusion.5
  94.3 0.8 constant_dynamic-update-slice_fusion.4
  95.0 0.8 constant_dynamic-update-slice_fusion.3
  95.8 0.8 constant_dynamic-update-slice_fusion.2
  96.6 0.8 constant_dynamic-update-slice_fusion.1
  97.4 0.8 constant_dynamic-update-slice_fusion
  98.2 8.1 %all-gather.5.cloned.1.call-done = bf16[7168,1024]{1,0:T(8,128)(2,1)} async-done(((bf16[1792,1024]{1,0:T(8,128)(2,1)}), bf16[7168,1024]{1,0:T(8,128)(2,1)}) %all-gather.5.cloned.1.call-update) | async-done | bytes 14680080 | tf_op jit(solution)/shard_map/all_gather | solution.py:36
  106.3 7.7 %select_reduce_fusion = (f32[192]{0:T(256)S(1)}, f32[192,1024]{1,0:T(8,128)S(1)}) fusion(pred[1024]{0:T(1024)(128)(4,1)S(1)} %broadcast_compare_fusion, bf16[7168,1024]{1,0:T(8,128)(2,1)} %all-gather.5.cloned.1.call-done, bf16[192,14336]{1,0:T(8,128)(2,1)} %constant_dynamic-update-slice_fusion, s32[]{:T(128)S(6)} %select_n.22), kind=kOutput, calls=%fused_computation.13 | convolution fusion | flops 2818965248 | bytes 18220804 | tf_op jit(solution)/shard_map/dot_general | solution.py:34
  115.2 37.0 %all-reduce.3 = (f32[1536]{0:T(1024)S(1)}, f32[1536]{0:T(1024)S(1)}, f32[1536]{0:T(1024)S(1)}) all-reduce(f32[1536]{0:T(1024)S(1)} %dynamic-update-slice, f32[1536]{0:T(1024)S(1)} %dynamic-update-slice.1, f32[1536]{0:T(1024)S(1)} %dynamic-update-slice.2), channel_id=2, replica_groups=mesh['vocab'=8,'tok'=4] {'vocab'}, use_global_device_ids=true, to_apply=%add | all-reduce | flops 4608 | bytes 36864
  153.8 12.6 %fusion.6 = f32[192,7168]{1,0:T(8,128)} fusion(bf16[7168,1024]{1,0:T(8,128)(2,1)} %all-gather.5.cloned.1.call-done, f32[192,1024]{1,0:T(8,128)S(1)} %get-tuple-element.70, f32[192]{0:T(256)S(1)} %get-tuple-element.66, s32[1024]{0:T(1024)S(1)} %iota_add_fusion, f32[192]{0:T(256)S(1)} %copy-done.2, s32[192]{0:T(256)S(1)} %copy-done.1, ...), kind=kOutput, calls=%fused_computation.14 | convolution fusion | flops 2819948544 | bytes 20978944 | tf_op jit(solution)/shard_map/dot_general | solution.py:55
  166.4 103.4 %reduce-scatter.2.cloned.1.call-done = f32[192,896]{1,0:T(8,128)} async-done(((f32[192,7168]{1,0:T(8,128)}), f32[192,896]{1,0:T(8,128)}) %reduce-scatter.2.cloned.1.call-update) | async-done | bytes 688144 | tf_op jit(solution)/shard_map/reduce_scatter | solution.py:61
  269.8 1.9 convert_element_type.11
  (63 shorter events, 3.9 us)
Async XLA Ops:
  7.2 84.0 %copy-start = (bf16[192,896]{1,0:T(8,128)(2,1)S(1)}, bf16[192,896]{1,0:T(8,128)(2,1)}, u32[]{:S(2)}) copy-start(bf16[192,896]{1,0:T(8,128)(2,1)} %param.7) | copy-start | bytes 1032196
  7.2 99.1 %all-gather.5.cloned.1.call-start = ((), (), s32[]{:S(2)}) async-start(), calls=%async_computation.1 | async-start | bytes 18350080 | tf_op jit(solution)/shard_map/all_gather | solution.py:36
  7.9 261.9 %reduce-scatter.2.cloned.1.call-start = ((), (), s32[]{:S(2)}) async-start(), calls=%async_computation.2 | async-start | bytes 6193152 | tf_op jit(solution)/shard_map/reduce_scatter | solution.py:61
  8.0 14.3 %collective-permute-start = (bf16[192,896]{1,0:T(8,128)(2,1)}, bf16[192,896]{1,0:T(8,128)(2,1)S(1)}, u32[]{:S(2)}, u32[]{:S(2)}) collective-permute-start(bf16[192,896]{1,0:T(8,128)(2,1)} %param.7), channel_id=1, source_target_pairs={{0,4},{4,8},{8,12},{12,16},{16,20},{20,24},{24,28},{28,0},{1,5},{5... | collective-permute-start | bytes 1032200 | tf_op jit(solution)/shard_map/ppermute | solution.py:26
  22.3 11.9 %collective-permute-start.1 = (bf16[192,896]{1,0:T(8,128)(2,1)S(1)}, bf16[192,896]{1,0:T(8,128)(2,1)S(1)}, u32[]{:S(2)}, u32[]{:S(2)}) collective-permute-start(bf16[192,896]{1,0:T(8,128)(2,1)S(1)} %collective-permute-done), channel_id=1, source_target_pairs={{0,4},{4,8},{8,12},{12,16},{16,20},{20,24},{24,28},{28,0},{1,5},{5... | collective-permute-start | bytes 1032200 | tf_op jit(solution)/shard_map/ppermute | solution.py:26
  34.2 11.1 %collective-permute-start.2 = (bf16[192,896]{1,0:T(8,128)(2,1)S(1)}, bf16[192,896]{1,0:T(8,128)(2,1)S(1)}, u32[]{:S(2)}, u32[]{:S(2)}) collective-permute-start(bf16[192,896]{1,0:T(8,128)(2,1)S(1)} %collective-permute-done.1), channel_id=1, source_target_pairs={{0,4},{4,8},{8,12},{12,16},{16,20},{20,24},{24,28},{28,0},{1,5},{5... | collective-permute-start | bytes 1032200 | tf_op jit(solution)/shard_map/ppermute | solution.py:26
  45.3 10.2 %collective-permute-start.3 = (bf16[192,896]{1,0:T(8,128)(2,1)S(1)}, bf16[192,896]{1,0:T(8,128)(2,1)S(1)}, u32[]{:S(2)}, u32[]{:S(2)}) collective-permute-start(bf16[192,896]{1,0:T(8,128)(2,1)S(1)} %collective-permute-done.2), channel_id=1, source_target_pairs={{0,4},{4,8},{8,12},{12,16},{16,20},{20,24},{24,28},{28,0},{1,5},{5... | collective-permute-start | bytes 1032200 | tf_op jit(solution)/shard_map/ppermute | solution.py:26
  55.5 9.9 %collective-permute-start.4 = (bf16[192,896]{1,0:T(8,128)(2,1)S(1)}, bf16[192,896]{1,0:T(8,128)(2,1)S(1)}, u32[]{:S(2)}, u32[]{:S(2)}) collective-permute-start(bf16[192,896]{1,0:T(8,128)(2,1)S(1)} %collective-permute-done.3), channel_id=1, source_target_pairs={{0,4},{4,8},{8,12},{12,16},{16,20},{20,24},{24,28},{28,0},{1,5},{5... | collective-permute-start | bytes 1032200 | tf_op jit(solution)/shard_map/ppermute | solution.py:26
  65.4 10.3 %collective-permute-start.5 = (bf16[192,896]{1,0:T(8,128)(2,1)S(1)}, bf16[192,896]{1,0:T(8,128)(2,1)S(1)}, u32[]{:S(2)}, u32[]{:S(2)}) collective-permute-start(bf16[192,896]{1,0:T(8,128)(2,1)S(1)} %collective-permute-done.4), channel_id=1, source_target_pairs={{0,4},{4,8},{8,12},{12,16},{16,20},{20,24},{24,28},{28,0},{1,5},{5... | collective-permute-start | bytes 1032200 | tf_op jit(solution)/shard_map/ppermute | solution.py:26
  75.7 9.9 %collective-permute-start.6 = (bf16[192,896]{1,0:T(8,128)(2,1)S(1)}, bf16[192,896]{1,0:T(8,128)(2,1)S(1)}, u32[]{:S(2)}, u32[]{:S(2)}) collective-permute-start(bf16[192,896]{1,0:T(8,128)(2,1)S(1)} %collective-permute-done.5), channel_id=1, source_target_pairs={{0,4},{4,8},{8,12},{12,16},{16,20},{20,24},{24,28},{28,0},{1,5},{5... | collective-permute-start | bytes 1032200 | tf_op jit(solution)/shard_map/ppermute | solution.py:26
  98.2 16.1 %copy-start.1 = (s32[192]{0:T(256)S(1)}, s32[192]{0:T(256)}, u32[]{:S(2)}) copy-start(s32[192]{0:T(256)} %param.9) | copy-start | bytes 2308
  98.2 55.6 %copy-start.2 = (f32[192]{0:T(256)S(1)}, f32[192]{0:T(256)}, u32[]{:S(2)}) copy-start(f32[192]{0:T(256)} %param.11) | copy-start | bytes 2308
Sparse Core Ops, SparseCore 0:
  9.5 96.7 all-gather.4
  166.5 103.2 reduce-scatter.1
